TPU v7x, 32 devices: a whole 2x2x4 slice. The times are simulated.
32 devices in a mesh: lat: 16 (over z, y, core), ma: 2 (over x).
Axes of the slice: x: 2, y: 2, z: 4, core: 2. Of those that a mesh axis runs over, the one named last changes fastest.
Arguments:
- pair_wave: int32 [360], replicated, may hold values from 0 to 359, each once
- legendre: bfloat16 [360, 160, 736], P('ma', 'lat'), may hold values from -0.0078125 to 0.0078125
- coefs: bfloat16 [360, 736, 168], P('ma', 'lat'), may hold values from -6 to 6
Outputs:
- noise: float32 [13440, 1440], P(('lat', 'ma'))
Inputs may be any that keep to these rules, and one draw needn't show every extreme that they name: Slot q holds wavenumbers pair_wave[q] and 719 - pair_wave[q]; every value appears once.
All inputs are finite; a program needn't handle non-finite values.
Results may differ from a plain program's by a relative error of at most 0.0003.
Values may be sent and summed in bfloat16 or wider, within the bound.
A program may use at most 64 MiB of HBM per device.

v0:
```python
import math

import jax
import jax.numpy as jnp
from jax import lax
from jax.sharding import PartitionSpec as P

DEG = 720
LON = 1440
CH = 84
LAT_DEV = 10


def chain_table(table, wave_ids, degree_top):
    row_count = table.shape[2]
    row_ids = jnp.arange(row_count, dtype=jnp.int32)[None, :]
    split_row = (degree_top - wave_ids)[:, None]
    inside = row_ids < split_row
    outside = (row_ids >= split_row) & (row_ids <= degree_top)
    masks = jnp.stack([inside, outside], axis=1)
    return jnp.where(masks[:, :, None, :], table[:, None, :, :], jnp.zeros((), table.dtype))


def fourier_basis(pair_wave, degree_top, lon_count):
    orders = jnp.stack([pair_wave, degree_top - 1 - pair_wave], axis=1)
    positions = jnp.arange(lon_count, dtype=jnp.int32)
    phase_int = orders[:, :, None] * positions[None, None, :] % lon_count
    radians = 2.0 * math.pi / lon_count * phase_int.astype(jnp.float32)
    weight = jnp.where(orders == 0, 1.0, 2.0).astype(jnp.float32)[:, :, None]
    real_row = weight * jnp.cos(radians)
    imag_row = -weight * jnp.sin(radians)
    return jnp.stack([real_row, imag_row], axis=2).reshape(-1, lon_count)


def body(pair_wave, legendre, coefs):
    lat_count = lax.axis_size("lat")
    lat_place = lax.axis_index("lat")
    ma_place = lax.axis_index("ma")
    slot_count = coefs.shape[0]
    wave_ids = lax.dynamic_slice_in_dim(pair_wave, ma_place * slot_count, slot_count)
    per_device = (slot_count + lat_count - 1) // lat_count
    extra = per_device * lat_count - slot_count
    table_pad = jnp.concatenate(
        [legendre, jnp.zeros((extra,) + legendre.shape[1:], legendre.dtype)], axis=0
    )
    coefs_pad = jnp.concatenate([coefs, jnp.zeros((extra,) + coefs.shape[1:], coefs.dtype)], axis=0)
    waves_pad = jnp.concatenate([wave_ids, jnp.zeros((extra,), jnp.int32)], axis=0)
    tables_in, coefs_in = (
        lax.all_to_all(table_pad, "lat", split_axis=0, concat_axis=1, tiled=True),
        lax.all_to_all(coefs_pad, "lat", split_axis=0, concat_axis=1, tiled=True),
    )
    my_waves = lax.dynamic_slice_in_dim(waves_pad, lat_place * per_device, per_device)
    masked = chain_table(tables_in, my_waves, DEG)
    sums = jnp.einsum("qeir,qrc->qeic", masked, coefs_in, preferred_element_type=jnp.float32)
    returned = lax.all_to_all(sums, "lat", split_axis=2, concat_axis=0, tiled=True)
    spectra = returned[:slot_count]
    arranged = jnp.transpose(
        spectra.reshape(slot_count, 2, LAT_DEV, 2, CH), (0, 1, 3, 2, 4)
    ).reshape(slot_count, 2, 2, LAT_DEV * CH)
    exchanged = lax.all_to_all(arranged, "ma", split_axis=3, concat_axis=0, tiled=True)
    fourier_rows = exchanged.reshape(-1, exchanged.shape[3])
    synth_basis = fourier_basis(pair_wave, DEG, LON)
    return lax.dot_general(
        fourier_rows, synth_basis, (((0,), (0,)), ((), ())), precision=lax.Precision.HIGHEST
    )


def solution(mesh):
    in_specs = (P(), P("ma", "lat", None), P("ma", "lat", None))
    out_specs = P(("lat", "ma"), None)
    return jax.shard_map(body, mesh=mesh, in_specs=in_specs, out_specs=out_specs, check_vma=False)
```

profile of v0, /device:TPU:18, one launch (start us, length us, event | category | flops | bytes accessed | tf_op | source)
XLA Modules:
  0.0 452.4 jit_solution(1085971635517473571)
XLA Ops:
  0.0 2.6 copy.61
  2.6 2.9 concatenate.17
  5.5 6.2 %all-to-all-start = ((bf16[192,10,736]{2,1,0:T(8,128)(2,1)}), bf16[192,10,736]{2,1,0:T(8,128)(2,1)}, u32[]{:S(2)}, u32[]{:S(2)}) async-start(bf16[192,10,736]{2,1,0:T(8,128)(2,1)} %concatenate.17), calls=%async_computation | async-start | bytes 9437184 | tf_op jit(solution)/shard_map/all_to_all | solution.py:49
  11.6 7.4 %copy.65 = bf16[180,46,168]{2,1,0:T(8,128)(2,1)} copy(bf16[180,46,168]{0,2,1:T(8,128)(2,1)} %param.5) | data formatting | bytes 5564160 | tf_op args[2]
  19.1 5.2 %concatenate.18 = bf16[192,46,168]{2,1,0:T(8,128)(2,1)} pad(bf16[180,46,168]{2,1,0:T(8,128)(2,1)} %copy.65, bf16[]{:T(256)} %constant.22.clone.1), padding=0_12x0_0x0_0 | pad | bytes 5749634 | tf_op jit(solution)/shard_map/concatenate | solution.py:46
  24.3 0.0 copy-start
  24.3 91.2 %all-to-all-done = bf16[192,10,736]{2,1,0:T(8,128)(2,1)} async-done(((bf16[192,10,736]{2,1,0:T(8,128)(2,1)}), bf16[192,10,736]{2,1,0:T(8,128)(2,1)}, u32[]{:S(2)}, u32[]{:S(2)}) %all-to-all-start) | async-done | bytes 2826272 | tf_op jit(solution)/shard_map/all_to_all | solution.py:49
  115.5 4.6 %all-to-all-start.1 = ((bf16[192,46,168]{2,1,0:T(8,128)(2,1)}), bf16[192,46,168]{2,1,0:T(8,128)(2,1)}, u32[]{:S(2)}, u32[]{:S(2)}) async-start(bf16[192,46,168]{2,1,0:T(8,128)(2,1)} %concatenate.18), calls=%async_computation.1 | async-start | bytes 9437184 | tf_op jit(solution)/shard_map/all_to_all | solution.py:50
  120.1 0.0 copy-done
  120.1 0.1 dynamic_slice.6
  120.2 0.1 fusion.10
  120.3 0.2 iota_compare_fusion
  120.4 0.1 pad_add_fusion
  120.6 3.7 copy.63
  124.2 0.9 copy.64
  125.2 98.8 %all-to-all-done.1 = bf16[192,46,168]{2,1,0:T(8,128)(2,1)} async-done(((bf16[192,46,168]{2,1,0:T(8,128)(2,1)}), bf16[192,46,168]{2,1,0:T(8,128)(2,1)}, u32[]{:S(2)}, u32[]{:S(2)}) %all-to-all-start.1) | async-done | bytes 2967584 | tf_op jit(solution)/shard_map/all_to_all | solution.py:50
  224.0 5.0 %copy.66 = bf16[12,16,46,168]{3,2,1,0:T(8,128)(2,1)} copy(bf16[12,16,46,168]{3,2,0,1:T(8,128)(2,1)} %bitcast.5) | data formatting | bytes 5935104 | tf_op jit(solution)/shard_map/all_to_all | solution.py:50
  229.0 7.7 %reshape.178 = bf16[12,736,168,1]{2,1,3,0:T(8,128)(2,1)} reshape(bf16[12,16,46,168]{3,2,1,0:T(8,128)(2,1)} %copy.66) | data formatting | bytes 5935104 | tf_op jit(solution)/shard_map/all_to_all | solution.py:50
  236.6 4.0 fusion
  240.6 4.9 %copy.68 = f32[12,2,160,168]{3,1,0,2:T(2,128)} copy(f32[12,2,160,168]{3,2,1,0:T(8,128)S(1)} %fusion) | data formatting | bytes 5160960 | tf_op jit(solution)/shard_map/qeir,qrc->qeic/dot_general | solution.py:54
  245.5 17.4 %all-to-all-start.2 = ((f32[12,2,160,168]{3,1,0,2:T(2,128)}), f32[12,2,160,168]{3,1,0,2:T(2,128)}, u32[]{:S(2)}, u32[]{:S(2)}) async-start(f32[12,2,160,168]{3,1,0,2:T(2,128)} %copy.68), calls=%async_computation.2 | async-start | bytes 7864320 | tf_op jit(solution)/shard_map/all_to_all | solution.py:55
  263.0 86.8 %all-to-all-done.2 = f32[12,2,160,168]{3,1,0,2:T(2,128)} async-done(((f32[12,2,160,168]{3,1,0,2:T(2,128)}), f32[12,2,160,168]{3,1,0,2:T(2,128)}, u32[]{:S(2)}, u32[]{:S(2)}) %all-to-all-start.2) | async-done | bytes 2580512 | tf_op jit(solution)/shard_map/all_to_all | solution.py:55
  349.8 4.0 copy.69
  353.8 1.3 slice.5
  355.1 3.7 copy.70
  358.8 7.1 %reshape.171 = f32[180,2,10,2,84]{4,3,1,2,0:T(2,128)} reshape(f32[15,12,2,10,168]{4,2,3,1,0:T(2,128)} %copy.70) | data formatting | bytes 4838400 | tf_op jit(solution)/shard_map/reshape | solution.py:58
  365.9 8.1 %copy.80 = f32[180,2,2,10,84]{0,2,1,4,3:T(2,128)} copy(f32[180,2,2,10,84]{4,2,1,3,0:T(2,128)} %bitcast.24) | data formatting | bytes 4838400 | tf_op jit(solution)/shard_map/reshape | solution.py:59
  374.0 5.9 %all-to-all-start.3 = ((f32[180,2,2,840]{0,2,1,3:T(2,128)}), f32[180,2,2,840]{0,2,1,3:T(2,128)}, u32[]{:S(2)}, u32[]{:S(2)}) async-start(f32[180,2,2,840]{0,2,1,3:T(2,128)} %bitcast.9), calls=%async_computation.3 | async-start | bytes 6881280 | tf_op jit(solution)/shard_map/all_to_all | solution.py:60
  379.9 18.8 %cosine_multiply_fusion = (f32[360,2,1,1440]{3,0,2,1:T(8,128)S(1)}, f32[360,2,1,1440]{3,0,2,1:T(8,128)S(1)}) fusion(s32[360,2]{0,1:T(2,128)S(1)} %pad_add_fusion.1, f32[360,2]{0,1:T(2,128)S(1)} %get-tuple-element.7, f32[360,2]{0,1:T(2,128)S(1)} %get-tuple-element.8), kind=kLoop, calls=%fused_computation.8 | loop fusion | flops 11404800 | bytes 8303040 | tf_op jit(solution)/shard_map/mul | solution.py:30
  398.7 1.0 pad_maximum_fusion
  399.8 10.9 %copy.75 = f32[360,2,2,1440]{3,2,1,0:T(2,128)} copy(f32[360,2,2,1440]{3,0,2,1:T(8,128)S(1)} %pad_maximum_fusion) | data formatting | bytes 16588800 | tf_op jit(solution)/shard_map/stack | solution.py:32
  410.7 11.4 %reshape.174 = f32[1440,1440]{1,0:T(8,128)} reshape(f32[360,2,2,1440]{3,2,1,0:T(2,128)} %copy.75) | data formatting | bytes 16588800 | tf_op jit(solution)/shard_map/reshape | solution.py:32
  422.1 0.0 all-to-all-done.3
  422.1 9.3 %copy.74 = f32[2,180,2,2,420]{4,3,2,1,0:T(2,128)S(1)} copy(f32[2,180,2,2,420]{1,3,2,4,0:T(2,128)} %bitcast.12) | data formatting | bytes 4838400 | tf_op jit(solution)/shard_map/all_to_all | solution.py:60
  431.4 3.3 reshape.173
  434.7 17.4 %fusion.13 = f32[420,1440]{1,0:T(8,128)} fusion(f32[1440,420]{1,0:T(8,128)} %reshape.173, f32[1440,1440]{1,0:T(8,128)} %reshape.174), kind=kOutput, calls=%fused_computation.26 | convolution fusion | flops 10450944000 | bytes 13132800 | tf_op jit(solution)/shard_map/dot_general | solution.py:63
  (6 shorter events, 0.0 us)
Async XLA Ops:
  5.5 110.1 %all-to-all-start = ((bf16[192,10,736]{2,1,0:T(8,128)(2,1)}), bf16[192,10,736]{2,1,0:T(8,128)(2,1)}, u32[]{:S(2)}, u32[]{:S(2)}) async-start(bf16[192,10,736]{2,1,0:T(8,128)(2,1)} %concatenate.17), calls=%async_computation | async-start | bytes 9437184 | tf_op jit(solution)/shard_map/all_to_all | solution.py:49
  24.3 95.8 %copy-start = (s32[360]{0:T(512)S(1)}, s32[360]{0:T(512)}, u32[]{:S(2)}) copy-start(s32[360]{0:T(512)} %param.3) | copy-start | bytes 4324
  115.5 108.5 %all-to-all-start.1 = ((bf16[192,46,168]{2,1,0:T(8,128)(2,1)}), bf16[192,46,168]{2,1,0:T(8,128)(2,1)}, u32[]{:S(2)}, u32[]{:S(2)}) async-start(bf16[192,46,168]{2,1,0:T(8,128)(2,1)} %concatenate.18), calls=%async_computation.1 | async-start | bytes 9437184 | tf_op jit(solution)/shard_map/all_to_all | solution.py:50
  245.5 104.3 %all-to-all-start.2 = ((f32[12,2,160,168]{3,1,0,2:T(2,128)}), f32[12,2,160,168]{3,1,0,2:T(2,128)}, u32[]{:S(2)}, u32[]{:S(2)}) async-start(f32[12,2,160,168]{3,1,0,2:T(2,128)} %copy.68), calls=%async_computation.2 | async-start | bytes 7864320 | tf_op jit(solution)/shard_map/all_to_all | solution.py:55
  374.0 48.0 %all-to-all-start.3 = ((f32[180,2,2,840]{0,2,1,3:T(2,128)}), f32[180,2,2,840]{0,2,1,3:T(2,128)}, u32[]{:S(2)}, u32[]{:S(2)}) async-start(f32[180,2,2,840]{0,2,1,3:T(2,128)} %bitcast.9), calls=%async_computation.3 | async-start | bytes 6881280 | tf_op jit(solution)/shard_map/all_to_all | solution.py:60
where the time goes:
time: 456 us; the launch traced here: 452 us
  waiting for transfers between devices  277 us (61%)
  local copies, waits for them, and re-layouts  99.4 us (22%)
  starting transfers between devices  34 us (7%)
  matrix products  21.4 us (5%)
  other arithmetic  20.2 us (4%)
    all_to_all x1, waiting for transfers between devices, body(): lax.all_to_all(coefs_pad, 'lat', split_axis=0, concat_axis=1, tiled=True)  98.8 us
    all_to_all x1, waiting for transfers between devices, body(): lax.all_to_all(table_pad, 'lat', split_axis=0, concat_axis=1, tiled=True)  91.2 us
    all_to_all x1, waiting for transfers between devices, body(): lax.all_to_all(sums, 'lat', split_axis=2, concat_axis=0, tiled=True)  86.8 us
    mul x1, other arithmetic, fourier_basis(): real_row = weight * jnp.cos(radians)  18.8 us
    all_to_all x1, starting transfers between devices, body(): lax.all_to_all(sums, 'lat', split_axis=2, concat_axis=0, tiled=True)  17.4 us
    dot_general x1, matrix products, body(): lax.dot_general(fourier_rows, synth_basis, (((0,), (0,)), ((), ())), prec...  17.4 us
    all_to_all x2, local copies, waits for them, and re-layouts, body(): lax.all_to_all(coefs_pad, 'lat', split_axis=0, concat_axis=1, tiled=True)  12.6 us
    reshape x1, local copies, waits for them, and re-layouts, fourier_basis(): return jnp.stack([real_row, imag_row], axis=2).reshape(-1, lon_count)  11.4 us
  transfers between devices with their start and end apart: 4, of which 3 were waited for; matrix products, arithmetic and copies ran while one was open for 13% of the time, Pallas kernels for 0%

commit v1 on v0

v1 whole, which is shorter than its diff:
```python
import math

import jax
import jax.numpy as jnp
from jax import lax
from jax.sharding import PartitionSpec as P

LON = 1440


def split_bf16(x):
    hi = lax.reduce_precision(x, 8, 7)
    return hi.astype(jnp.bfloat16), (x - hi).astype(jnp.bfloat16)


def basis_rows(waves, quarter, lon_count):
    positions = jnp.arange(lon_count, dtype=jnp.int32)
    phase = (waves[:, None] * positions[None, :] + quarter[:, None]) % lon_count
    radians = 2.0 * math.pi / lon_count * phase.astype(jnp.float32)
    weight = jnp.where(waves == 0, 1.0, 2.0).astype(jnp.float32)[:, None]
    return split_bf16(weight * jnp.cos(radians))


def dot_rows(rows, basis):
    return lax.dot_general(
        rows, basis, (((0,), (0,)), ((), ())), preferred_element_type=jnp.float32
    )


def body(pair_wave, legendre, coefs):
    lat_n = lax.axis_size("lat")
    ma_n = lax.axis_size("ma")
    lat_i = lax.axis_index("lat")
    ma_i = lax.axis_index("ma")
    slots, rows_dev, row_count = legendre.shape
    deg_dev, cols = coefs.shape[1:]
    ch = cols // 2
    degree_top = 2 * pair_wave.shape[0]
    per = -(-slots // lat_n)
    per += -per % 2
    padded = per * lat_n
    waves = jnp.pad(pair_wave.reshape(ma_n, slots), ((0, 0), (0, padded - slots)))
    waves = waves.reshape(ma_n, lat_n, per)

    order = waves.transpose(1, 0, 2).reshape(-1, 1, 1, per)
    order = jnp.concatenate([order, degree_top - 1 - order], axis=2)
    order = jnp.broadcast_to(order, (lat_n * ma_n, 2, 2, per))
    quarter = jnp.arange(2, dtype=jnp.int32)[None, :, None, None] * (LON // 4)
    quarter = jnp.broadcast_to(quarter, order.shape)
    b_hi, b_lo = basis_rows(order.reshape(-1), quarter.reshape(-1), LON)

    table = jnp.transpose(legendre, (1, 0, 2))
    table = jnp.pad(table, ((0, 0), (0, padded - slots), (0, 0)))
    table = table.reshape(rows_dev, lat_n, per, row_count).transpose(1, 0, 2, 3)
    table = table.reshape(lat_n, rows_dev * per, row_count)
    table = lax.all_to_all(table, "lat", split_axis=0, concat_axis=0, tiled=True)
    table = table.reshape(lat_n * rows_dev, per, row_count).transpose(1, 0, 2)

    full = cols // 128 * 128
    rest = cols - full
    group = 1
    for g in range(1, 128 // rest + 1):
        if per % g == 0:
            group = g
    packed = jnp.pad(coefs, ((0, padded - slots), (0, 0), (0, 0)))
    packed = packed.reshape(lat_n, per, deg_dev, cols)
    head = packed[..., :full].reshape(lat_n, per * deg_dev, full)
    tail = packed[..., full:].reshape(lat_n, group, per // group, deg_dev, rest)
    tail = jnp.concatenate([tail[:, g] for g in range(group)], axis=-1)
    tail = tail.reshape(lat_n, per // group * deg_dev, group * rest)
    tail = jnp.pad(tail, ((0, 0), (0, 0), (0, 128 - group * rest)))
    both = jnp.concatenate([head, tail], axis=1)
    both = lax.all_to_all(both, "lat", split_axis=0, concat_axis=0, tiled=True)
    both, b_hi, b_lo = lax.optimization_barrier((both, b_hi, b_lo))
    head = both[:, : per * deg_dev].reshape(lat_n, per, deg_dev, full)
    tail = both[:, per * deg_dev :].reshape(lat_n, per // group, deg_dev, 128)
    tail = jnp.concatenate(
        [tail[..., g * rest : (g + 1) * rest] for g in range(group)], axis=1
    )
    mine = jnp.concatenate([head, tail], axis=-1)
    mine = mine.transpose(1, 0, 2, 3).reshape(per, row_count, cols)

    my_waves = waves[ma_i, lat_i]
    row_ids = jnp.arange(row_count, dtype=jnp.int32)[None, :]
    split_row = (degree_top - my_waves)[:, None]
    inside = row_ids < split_row
    outside = (row_ids >= split_row) & (row_ids <= degree_top)
    masks = jnp.stack([inside, outside], axis=1)
    masked = jnp.where(masks[:, :, None, :], table[:, None], jnp.zeros((), table.dtype))
    sums = jnp.einsum("qhir,qrc->qhic", masked, mine, preferred_element_type=jnp.float32)

    places = lat_n * ma_n
    width = rows_dev * ch // ma_n
    sums = sums.reshape(per, 2, lat_n, rows_dev, 2, ch).transpose(2, 4, 1, 0, 3, 5)
    sums = sums.reshape(lat_n, 4 * per, ma_n, width).transpose(0, 2, 1, 3)
    top = jnp.max(jnp.abs(sums), axis=3, keepdims=True)
    power = jnp.ceil(jnp.log2(jnp.maximum(top, 1e-30)) + 1e-3)
    coded = jnp.round(sums * (jnp.exp2(-power) * 32767.0)).astype(jnp.int16)
    coded = jnp.concatenate([coded, power.astype(jnp.int16)], axis=3)
    coded = coded.reshape(places, 4 * per, width + 1)
    coded = lax.all_to_all(coded, ("lat", "ma"), split_axis=0, concat_axis=0, tiled=True)
    spectra = coded[..., :width].astype(jnp.float32)
    scale = jnp.exp2(coded[..., width:].astype(jnp.float32)) * (1.0 / 32767.0)
    spectra = (spectra * scale).reshape(places * 4 * per, width)
    f_hi, f_lo = split_bf16(spectra)
    return dot_rows(f_hi, b_hi) + (dot_rows(f_hi, b_lo) + dot_rows(f_lo, b_hi))


def solution(mesh):
    in_specs = (P(), P("ma", "lat", None), P("ma", "lat", None))
    out_specs = P(("lat", "ma"), None)
    return jax.shard_map(body, mesh=mesh, in_specs=in_specs, out_specs=out_specs, check_vma=False)
```

time: 456 us -> 258 us (0.57)
  waiting for transfers between devices: 277 us -> 43.2 us
  blocking collectives: 0 us -> 39.9 us
  other arithmetic: 20.2 us -> 49.8 us
  starting transfers between devices: 34 us -> 10.8 us
  local copies, waits for them, and re-layouts: 99.4 us -> 92.1 us
  matrix products: 21.4 us -> 16.7 us
    all_to_all x4 -> x2, waiting for transfers between devices: 277 us -> 43.2 us  [the longest x1 29.7 us: body(): lax.all_to_all(table, 'lat', split_axis=0, concat_axis=0, tiled=True)]
    convert_element_type x0 -> x3, other arithmetic: none -> 44.4 us  [the longest x2 42.4 us: split_bf16(): return (hi.astype(jnp.bfloat16), (x - hi).astype(jnp.bfloat16))]
    all_to_all x0 -> x1, blocking collectives: none -> 39.9 us  [body(): lax.all_to_all(coded, ('lat', 'ma'), split_axis=0, concat_axis=0, tiled=T...]
    all_to_all x5 -> x0, local copies, waits for them, and re-layouts: 29.6 us -> none  [the longest x2 12.6 us: body(): lax.all_to_all(coefs_pad, 'lat', split_axis=0, concat_axis=1, tiled=True)]
    all_to_all x4 -> x2, starting transfers between devices: 34 us -> 10.8 us  [the longest x1 6.18 us: body(): lax.all_to_all(table, 'lat', split_axis=0, concat_axis=0, tiled=True)]
    mul x1 -> x4, other arithmetic: 18.8 us -> 0.59 us  [the longest x2 0.56 us: body(): spectra = (spectra * scale).reshape(places * 4 * per, width)]
    transpose x0 -> x4, local copies, waits for them, and re-layouts: none -> 12 us  [the longest x1 4.65 us: body(): table = table.reshape(lat_n * rows_dev, per, row_count).transpose(1, 0, 2)]
    another operation x3 -> x0, local copies, waits for them, and re-layouts: 11 us -> none  [the longest x1 10.9 us: fourier_basis(): return jnp.stack([real_row, imag_row], axis=2).reshape(-1, lon_count)]
  transfers between devices with their start and end apart: 4 -> 2, of which waited for: 3 -> 2; matrix products, arithmetic and copies ran while one was open for 13% -> 36% of each run, Pallas kernels for 0% -> 0%
where the time goes in v1:
time: 258 us; the launch traced here: 253 us
  local copies, waits for them, and re-layouts  92.1 us (36%)
  other arithmetic  49.8 us (19%)
  waiting for transfers between devices  43.2 us (17%)
  blocking collectives  39.9 us (15%)
  matrix products  16.7 us (6%)
  starting transfers between devices  10.8 us (4%)
    convert_element_type x2, other arithmetic, split_bf16(): return (hi.astype(jnp.bfloat16), (x - hi).astype(jnp.bfloat16))  42.4 us
    all_to_all x1, blocking collectives, body(): lax.all_to_all(coded, ('lat', 'ma'), split_axis=0, concat_axis=0, tiled=T...  39.9 us
    all_to_all x1, waiting for transfers between devices, body(): lax.all_to_all(table, 'lat', split_axis=0, concat_axis=0, tiled=True)  29.7 us
    all_to_all x1, waiting for transfers between devices, body(): both = lax.all_to_all(both, 'lat', split_axis=0, concat_axis=0, tiled=True)  13.4 us
    reshape x2, local copies, waits for them, and re-layouts, body(): sums.reshape(per, 2, lat_n, rows_dev, 2, ch).transpose(2, 4, 1, 0, 3, 5)  11.6 us
    dot_general x3, matrix products, dot_rows(): lax.dot_general(rows, basis, (((0,), (0,)), ((), ())), preferred_element_...  10.9 us
    unnamed x18, local copies, waits for them, and re-layouts  9.32 us
    concatenate x3, local copies, waits for them, and re-layouts, body(): tail = jnp.concatenate([tail[:, g] for g in range(group)], axis=-1)  8 us
  transfers between devices with their start and end apart: 2, of which 2 were waited for; matrix products, arithmetic and copies ran while one was open for 36% of the time, Pallas kernels for 0%

profile of v1, /device:TPU:18, one launch (start us, length us, event | category | flops | bytes accessed | tf_op | source)
XLA Modules:
  0.0 252.8 jit_solution(14297552692107274321)
XLA Ops:
  0.0 2.1 pad.17
  2.1 3.2 %reshape.228 = bf16[10,16,12,736]{3,2,1,0:T(8,128)(2,1)} reshape(bf16[10,192,736]{2,1,0:T(8,128)(2,1)S(1)} %pad.17) | data formatting | bytes 5652480 | tf_op jit(solution)/shard_map/reshape | solution.py:54
  5.3 3.2 %copy.106 = bf16[16,10,12,736]{3,0,2,1:T(8,128)(2,1)S(1)} copy(bf16[16,10,12,736]{3,2,0,1:T(8,128)(2,1)} %bitcast.53) | data formatting | bytes 5652480 | tf_op jit(solution)/shard_map/transpose | solution.py:54
  8.5 2.6 %copy.107 = bf16[16,120,736]{2,1,0:T(8,128)(2,1)} copy(bf16[16,120,736]{2,0,1:T(8,128)(2,1)S(1)} %bitcast.56) | data formatting | bytes 5652480 | tf_op jit(solution)/shard_map/reshape | solution.py:55
  11.1 6.2 %all-to-all-start = ((bf16[16,120,736]{2,1,0:T(8,128)(2,1)}), bf16[16,120,736]{2,1,0:T(8,128)(2,1)S(1)}, u32[]{:S(2)}, u32[]{:S(2)}) async-start(bf16[16,120,736]{2,1,0:T(8,128)(2,1)} %copy.107), calls=%async_computation | async-start | bytes 5898240 | tf_op jit(solution)/shard_map/all_to_all | solution.py:56
  17.3 7.4 %copy.145 = bf16[180,46,168]{2,1,0:T(8,128)(2,1)} copy(bf16[180,46,168]{0,2,1:T(8,128)(2,1)} %param.5) | data formatting | bytes 5564160
  24.6 3.1 %pad.18.clone = bf16[192,46,168]{2,1,0:T(8,128)(2,1)S(1)} pad(bf16[180,46,168]{2,1,0:T(8,128)(2,1)} %copy.145, bf16[]{:T(256)} %constant.26.clone.1), padding=0_12x0_0x0_0 | pad | bytes 5749634 | tf_op jit(solution)/shard_map/jit(_pad)/pad | solution.py:65
  27.7 1.8 slice.49
  29.5 1.9 slice.48
  31.4 4.3 %copy.111 = bf16[16,12,46,40]{2,3,1,0:T(8,128)(2,1)} copy(bf16[16,12,46,40]{3,2,1,0:T(8,128)(2,1)} %slice.49) | data formatting | bytes 1413120 | tf_op jit(solution)/shard_map/slice | solution.py:68
  35.7 2.9 %fusion.29 = (bf16[16,1,4,46,40]{3,4,2,1,0:T(8,128)(2,1)}, bf16[16,1,4,46,40]{3,4,2,1,0:T(8,128)(2,1)}, bf16[16,1,4,46,40]{3,4,2,1,0:T(8,128)(2,1)}) fusion(bf16[16,3,4,46,40]{3,4,2,1,0:T(8,128)(2,1)} %bitcast.59), kind=kLoop, calls=%fused_computation.56 | loop fusion | bytes 1413120 | tf_op jit(solution)/shard_map/slice | solution.py:69
  38.6 2.7 %copy.138 = bf16[16,1,4,46,40]{4,0,3,2,1:T(8,128)(2,1)} copy(bf16[16,1,4,46,40]{3,4,2,1,0:T(8,128)(2,1)} %get-tuple-element.14) | data formatting | bytes 471040 | tf_op jit(solution)/shard_map/concatenate | solution.py:69
  41.3 2.7 %copy.136 = bf16[16,1,4,46,40]{4,0,3,2,1:T(8,128)(2,1)} copy(bf16[16,1,4,46,40]{3,4,2,1,0:T(8,128)(2,1)} %get-tuple-element.13) | data formatting | bytes 471040 | tf_op jit(solution)/shard_map/concatenate | solution.py:69
  43.9 2.7 %copy.137 = bf16[16,1,4,46,40]{4,0,3,2,1:T(8,128)(2,1)} copy(bf16[16,1,4,46,40]{3,4,2,1,0:T(8,128)(2,1)} %get-tuple-element.15) | data formatting | bytes 471040 | tf_op jit(solution)/shard_map/concatenate | solution.py:69
  46.6 3.3 %copy.110 = bf16[16,12,46,128]{3,0,2,1:T(8,128)(2,1)S(1)} copy(bf16[16,12,46,128]{3,2,1,0:T(8,128)(2,1)} %slice.48) | data formatting | bytes 4521984 | tf_op jit(solution)/shard_map/slice | solution.py:67
  49.9 0.0 copy-done.1
  49.9 0.0 copy-done.2
  49.9 0.0 copy-done.3
  49.9 0.8 fusion.22
  50.8 0.3 pad_maximum_fusion
  51.0 2.4 copy.118
  53.4 29.7 %all-to-all-done = bf16[16,120,736]{2,1,0:T(8,128)(2,1)S(1)} async-done(((bf16[16,120,736]{2,1,0:T(8,128)(2,1)}), bf16[16,120,736]{2,1,0:T(8,128)(2,1)S(1)}, u32[]{:S(2)}, u32[]{:S(2)}) %all-to-all-start) | async-done | bytes 2826272 | tf_op jit(solution)/shard_map/all_to_all | solution.py:56
  83.2 1.6 copy-done
  84.8 4.6 %all-to-all-start.1 = ((bf16[16,736,128]{2,1,0:T(8,128)(2,1)}), bf16[16,736,128]{2,1,0:T(8,128)(2,1)S(1)}, u32[]{:S(2)}, u32[]{:S(2)}) async-start(bf16[16,736,128]{2,1,0:T(8,128)(2,1)} %copy.118), calls=%async_computation.1 | async-start | bytes 6029312 | tf_op jit(solution)/shard_map/all_to_all | solution.py:73
  89.4 0.0 copy-done.5
  89.4 0.1 reshape.226
  89.5 0.1 reshape.227
  89.6 0.1 copy.120
  89.7 0.1 copy.121
  89.8 0.1 copy.122
  89.9 0.1 reshape.235
  90.0 0.1 broadcast_in_dim.55
  90.1 0.1 add.60
  90.3 0.2 iota_compare_fusion.1
  90.4 0.1 pad_add_fusion.1
  90.6 41.8 %fusion = (bf16[1536,1440]{1,0:T(8,128)(2,1)}, bf16[1536,1440]{1,0:T(8,128)(2,1)}) fusion(s32[1536]{0:T(1024)S(1)} %add.60, s32[1536]{0:T(1024)S(1)} %reshape.235, f32[1536]{0:T(1024)S(1)} %compare_select_fusion), kind=kLoop, calls=%fused_computation.3 | loop fusion | flops 33177600 | bytes 8865792 | tf_op jit(solution)/shard_map/convert_element_type | solution.py:13
  132.4 6.2 %reshape.230 = bf16[160,12,736]{2,1,0:T(8,128)(2,1)} reshape(bf16[16,120,736]{2,1,0:T(8,128)(2,1)} %copy-done) | data formatting | bytes 5652480 | tf_op jit(solution)/shard_map/reshape | solution.py:57
  138.6 4.7 %copy.108 = bf16[12,160,736]{2,1,0:T(8,128)(2,1)} copy(bf16[12,160,736]{2,0,1:T(8,128)(2,1)} %bitcast.54) | data formatting | bytes 5652480 | tf_op jit(solution)/shard_map/transpose | solution.py:57
  143.2 13.4 %all-to-all-done.1 = bf16[16,736,128]{2,1,0:T(8,128)(2,1)S(1)} async-done(((bf16[16,736,128]{2,1,0:T(8,128)(2,1)}), bf16[16,736,128]{2,1,0:T(8,128)(2,1)S(1)}, u32[]{:S(2)}, u32[]{:S(2)}) %all-to-all-start.1) | async-done | bytes 3014688 | tf_op jit(solution)/shard_map/all_to_all | solution.py:73
  156.6 1.2 copy.123
  157.8 0.1 slice.54
  158.0 0.4 slice.53
  158.3 0.5 fusion.30
  158.9 1.0 maximum_bitcast_fusion
  159.9 4.1 %copy.125 = bf16[12,16,46,168]{3,2,1,0:T(8,128)(2,1)} copy(bf16[12,16,46,168]{3,1,2,0:T(8,128)(2,1)S(1)} %maximum_bitcast_fusion) | data formatting | bytes 5935104 | tf_op jit(solution)/shard_map/transpose | solution.py:81
  164.0 7.7 %reshape.247 = bf16[12,736,168,1]{2,1,3,0:T(8,128)(2,1)} reshape(bf16[12,16,46,168]{3,2,1,0:T(8,128)(2,1)} %copy.125) | data formatting | bytes 5935104 | tf_op jit(solution)/shard_map/reshape | solution.py:81
  171.8 5.8 %fusion.8 = f32[12,2,160,168]{3,2,1,0:T(8,128)} fusion(bf16[12,736,168,1]{2,1,3,0:T(8,128)(2,1)} %reshape.247, pred[12,2,736]{2,1,0:T(4,128)(4,1)S(1)} %pad_add_fusion.1, bf16[12,160,736]{2,1,0:T(8,128)(2,1)S(1)} %copy-done.4), kind=kOutput, calls=%fused_computation.13 | convolution fusion | flops 952442880 | bytes 8391936 | tf_op jit(solution)/shard_map/qhir,qrc->qhic/dot_general | solution.py:90
  177.6 6.0 %reshape.239 = f32[12,2,16,10,2,84]{5,4,3,2,1,0:T(2,128)} reshape(f32[12,2,160,168]{3,2,1,0:T(8,128)} %fusion.8) | data formatting | bytes 5160960 | tf_op jit(solution)/shard_map/reshape | solution.py:94
  183.6 5.6 %copy.163 = f32[12,2,16,10,2,84]{5,3,0,1,4,2:T(8,128)} copy(f32[12,2,16,10,2,84]{5,4,3,2,1,0:T(2,128)} %reshape.239) | data formatting | bytes 5160960 | tf_op jit(solution)/shard_map/reshape | solution.py:94
  189.2 6.1 %reshape.240 = f32[16,48,2,420]{3,2,1,0:T(2,128)S(1)} reshape(f32[16,2,2,12,10,84]{5,4,3,2,1,0:T(8,128)} %bitcast.50) | data formatting | bytes 5160960 | tf_op jit(solution)/shard_map/reshape | solution.py:95
  195.3 0.7 fusion.12
  196.0 2.0 fusion.14
  198.1 0.4 copy.133
  198.5 1.7 pad_add_fusion
  200.2 39.9 %all_to_all.15 = s16[32,48,421]{2,1,0:T(8,128)(2,1)S(1)} all-to-all(s16[32,48,421]{2,1,0:T(8,128)(2,1)S(1)} %pad_add_fusion), channel_id=1, replica_groups=mesh['lat'=16,'ma'=2] {'lat','ma'}, dimensions={0} | all-to-all | bytes 2586624 | tf_op jit(solution)/shard_map/all_to_all | solution.py:101
  240.1 0.3 slice.59
  240.4 0.3 copy.144
  240.7 0.5 convert_multiply_fusion
  241.3 0.0 slice-start
  241.3 0.6 fusion.11
  241.9 0.0 slice-start.1
  241.9 4.9 %fusion.32 = f32[420,1440]{1,0:T(8,128)S(1)} fusion(bf16[1536,420]{1,0:T(8,128)(2,1)S(1)} %get-tuple-element.12, bf16[1536,1440]{1,0:T(8,128)(2,1)} %get-tuple-element.10), kind=kOutput, calls=%fused_computation.59 | convolution fusion | flops 1857945600 | bytes 8133120 | tf_op jit(solution)/shard_map/dot_general | solution.py:25
  246.8 2.2 fusion.31
  249.0 3.8 %fusion.15 = f32[420,1440]{1,0:T(8,128)} fusion(f32[420,1440]{1,0:T(8,128)S(1)} %fusion.31, f32[420,1440]{1,0:T(8,128)S(1)} %fusion.32, bf16[1536,420]{1,0:T(8,128)(2,1)S(1)} %get-tuple-element.11, bf16[1536,1440]{1,0:T(8,128)(2,1)S(1)} %bitcast.49), kind=kOutput, calls=%fused_computation.27 | convolution fusion | flops 1859155200 | bytes 12971520 | tf_op jit(solution)/shard_map/dot_general | solution.py:25
  (23 shorter events, 0.2 us)
Async XLA Ops:
  11.1 72.1 %all-to-all-start = ((bf16[16,120,736]{2,1,0:T(8,128)(2,1)}), bf16[16,120,736]{2,1,0:T(8,128)(2,1)S(1)}, u32[]{:S(2)}, u32[]{:S(2)}) async-start(bf16[16,120,736]{2,1,0:T(8,128)(2,1)} %copy.107), calls=%async_computation | async-start | bytes 5898240 | tf_op jit(solution)/shard_map/all_to_all | solution.py:56
  46.6 3.3 %copy-start.1 = (bf16[16,1,4,46,40]{4,0,3,2,1:T(8,128)(2,1)S(1)}, bf16[16,1,4,46,40]{4,0,3,2,1:T(8,128)(2,1)}, u32[]{:S(2)}) copy-start(bf16[16,1,4,46,40]{4,0,3,2,1:T(8,128)(2,1)} %copy.138) | copy-start | bytes 706564
  46.6 3.3 %copy-start.2 = (bf16[16,1,4,46,40]{4,0,3,2,1:T(8,128)(2,1)S(1)}, bf16[16,1,4,46,40]{4,0,3,2,1:T(8,128)(2,1)}, u32[]{:S(2)}) copy-start(bf16[16,1,4,46,40]{4,0,3,2,1:T(8,128)(2,1)} %copy.136) | copy-start | bytes 706564
  46.6 3.3 %copy-start.3 = (bf16[16,1,4,46,40]{4,0,3,2,1:T(8,128)(2,1)S(1)}, bf16[16,1,4,46,40]{4,0,3,2,1:T(8,128)(2,1)}, u32[]{:S(2)}) copy-start(bf16[16,1,4,46,40]{4,0,3,2,1:T(8,128)(2,1)} %copy.137) | copy-start | bytes 706564
  53.4 36.0 %copy-start.5 = (s32[360]{0:T(512)S(1)}, s32[360]{0:T(512)}, u32[]{:S(2)}) copy-start(s32[360]{0:T(512)} %param.3) | copy-start | bytes 4324
  83.2 1.6 copy-start
  84.8 71.9 %all-to-all-start.1 = ((bf16[16,736,128]{2,1,0:T(8,128)(2,1)}), bf16[16,736,128]{2,1,0:T(8,128)(2,1)S(1)}, u32[]{:S(2)}, u32[]{:S(2)}) async-start(bf16[16,736,128]{2,1,0:T(8,128)(2,1)} %copy.118), calls=%async_computation.1 | async-start | bytes 6029312 | tf_op jit(solution)/shard_map/all_to_all | solution.py:73
  164.0 7.8 %copy-start.4 = (bf16[12,160,736]{2,1,0:T(8,128)(2,1)S(1)}, bf16[12,160,736]{2,1,0:T(8,128)(2,1)}, u32[]{:S(2)}) copy-start(bf16[12,160,736]{2,1,0:T(8,128)(2,1)} %copy.108) | copy-start | bytes 8478724
  241.3 5.5 %slice-start = ((s8[4718592]{0:T(1024)(128)(4,1)}), s8[4194304]{0:T(1024)(128)(4,1)S(1)}, s32[]{:S(2)}) async-start(s8[4718592]{0:T(1024)(128)(4,1)} %bitcast.48), calls=%async_computation.3 | async-start | bytes 8388608
  241.9 4.9 %slice-start.1 = ((s8[4718592]{0:T(1024)(128)(4,1)}), s8[524288]{0:T(1024)(128)(4,1)S(1)}, s32[]{:S(2)}) async-start(s8[4718592]{0:T(1024)(128)(4,1)} %bitcast.48), calls=%async_computation.4 | async-start | bytes 1048576
